TPU v7x, 32 devices: a whole 2x2x4 slice. The times are simulated.
32 devices in a mesh: kv: 4 (over y, x), seq: 8 (over z, core).
Axes of the slice: x: 2, y: 2, z: 4, core: 2. Of those that a mesh axis runs over, the one named last changes fastest.
Arguments:
- queries: bfloat16 [2048, 16384], P('seq', 'kv'), may hold values from -24 to 24
- keys: bfloat16 [2048, 1024], P('seq', 'kv'), may hold values from -24 to 24
- values: bfloat16 [2048, 1024], P('seq', 'kv'), may hold values from -6 to 6
- query_map: float32 [128, 128, 64], P('kv'), may hold values from -4 to 4
- key_map: float32 [128, 128, 64], P('kv'), may hold values from -4 to 4
Outputs:
- grad_query_map: float32 [128, 128, 64], P(('kv', 'seq'))
- grad_key_map: float32 [128, 128, 64], P(('kv', 'seq'))
All inputs are finite; a program needn't handle non-finite values.
Results may differ from a plain program's by a relative error of at most 0.00165.
Values may be sent and summed in bfloat16 or wider, within the bound.
A program may use at most 128 MiB of HBM per device.

v0:
```python
import jax
import jax.numpy as jnp
from jax import lax
from jax.sharding import PartitionSpec as P

HD = 128


def block_size(count):
    return max((d for d in range(1, min(count, 512) + 1) if count % d == 0))


def feature(logits):
    return jnp.concatenate(
        [jax.nn.softmax(logits, axis=-1), jax.nn.softmax(-logits, axis=-1)], axis=-1
    )


def feature_back(phi, dphi, width):
    first, second = (phi[..., :width], phi[..., width:])
    dfirst, dsecond = (dphi[..., :width], dphi[..., width:])
    part_one = first * (dfirst - jnp.sum(first * dfirst, axis=-1, keepdims=True))
    part_two = second * (dsecond - jnp.sum(second * dsecond, axis=-1, keepdims=True))
    return part_one - part_two


def shards(queries, keys, values, query_map, key_map):
    tok = queries.shape[0]
    heads_dev = queries.shape[1] // HD
    kv_dev = keys.shape[1] // HD
    group = heads_dev // kv_dev
    width = query_map.shape[2]
    hi = lax.Precision.HIGHEST
    position = lax.axis_index("seq")
    length = tok * lax.axis_size("seq")
    scale = 1.0 / HD**0.5
    qpos = position * tok + jnp.arange(tok, dtype=jnp.int32)
    qlast = position * tok + tok - 1
    qgrouped = queries.reshape(tok, kv_dev, group, HD)

    def teacher_block(carry, kblock, vblock, kstart):
        running, total, acc = carry
        blk = kblock.shape[0]
        scores = (
            jnp.einsum("tgjd,sgd->gjts", qgrouped, kblock, preferred_element_type=jnp.float32)
            * scale
        )
        kpos = kstart + jnp.arange(blk, dtype=jnp.int32)
        allowed = (kpos[None, :] <= qpos[:, None])[None, None]
        newmax = jnp.maximum(running, jnp.max(jnp.where(allowed, scores, -1e30), axis=-1))
        probs = jnp.where(allowed, jnp.exp(scores - newmax[..., None]), 0.0)
        factor = jnp.exp(running - newmax)
        total = total * factor + jnp.sum(probs, axis=-1)
        acc = acc * factor[..., None] + jnp.einsum(
            "gjts,sgd->gjtd", probs, vblock.astype(jnp.float32), precision=hi
        )
        return (newmax, total, acc)

    def fold_keys(carry, piece, start):
        kpiece, vpiece = piece
        rows = kpiece.shape[0]
        blk = block_size(rows)
        kpiece = kpiece.reshape(rows // blk, blk, kv_dev, HD)
        vpiece = vpiece.reshape(rows // blk, blk, kv_dev, HD)

        def step(index, state):
            kstart = start + index * blk
            return lax.cond(
                kstart <= qlast,
                lambda inner: teacher_block(inner, kpiece[index], vpiece[index], kstart),
                lambda inner: inner,
                state,
            )

        return lax.fori_loop(0, rows // blk, step, carry)

    qheads = queries.reshape(tok, heads_dev, HD)
    start = (
        jnp.full((kv_dev, group, tok), -1e30, jnp.float32),
        jnp.zeros((kv_dev, group, tok), jnp.float32),
        jnp.zeros((kv_dev, group, tok, HD), jnp.float32),
    )
    running, total, acc = fold_keys(
        start,
        (
            lax.all_gather(keys, "seq", axis=0, tiled=True),
            lax.all_gather(values, "seq", axis=0, tiled=True),
        ),
        jnp.int32(0),
    )
    mixed = acc / total[..., None]
    teacher_out = mixed.transpose(2, 0, 1, 3).reshape(tok, heads_dev, HD).astype(jnp.bfloat16)
    k_student = keys.reshape(tok, kv_dev, HD)
    v_student = values.reshape(tok, kv_dev, HD)
    rows = tok
    head_kv = jnp.arange(heads_dev, dtype=jnp.int32) // group
    select = (head_kv[:, None] == jnp.arange(kv_dev, dtype=jnp.int32)[None, :]).astype(jnp.float32)
    khead = jnp.einsum("tgd,cg->tcd", k_student.astype(jnp.float32), select, precision=hi)
    vhead = jnp.einsum("tgd,cg->tcd", v_student.astype(jnp.float32), select, precision=hi)
    qfloat = qheads.astype(jnp.float32)
    fq = feature(jnp.einsum("tcd,cdf->tcf", qfloat, query_map, precision=hi))
    fk = feature(jnp.einsum("tcd,cdf->tcf", khead, key_map, precision=hi))
    lower = (jnp.arange(rows)[:, None] >= jnp.arange(rows)[None, :]).astype(jnp.float32)
    state_local = jnp.einsum("tcf,tcd->cfd", fk, vhead, precision=hi)
    norm_local = jnp.sum(fk, axis=0)

    def pick_rows(before, piece):
        count = piece[0].shape[0]
        source = jnp.arange(count, dtype=jnp.int32)
        if before:
            keep = source < position
        else:
            keep = source > position
        weight = keep.astype(jnp.float32)
        return (
            jnp.sum(weight[:, None, None, None] * piece[0], axis=0),
            jnp.sum(weight[:, None, None] * piece[1], axis=0),
        )

    state_prev, norm_prev = pick_rows(
        True,
        (
            lax.all_gather(state_local[None], "seq", axis=0, tiled=True),
            lax.all_gather(norm_local[None], "seq", axis=0, tiled=True),
        ),
    )
    attn = jnp.einsum("tcf,scf->cts", fq, fk, precision=hi) * lower[None]
    numer = jnp.einsum("cts,scd->tcd", attn, vhead, precision=hi) + jnp.einsum(
        "tcf,cfd->tcd", fq, state_prev, precision=hi
    )
    denom = jnp.sum(attn, axis=-1).T + jnp.einsum("tcf,cf->tc", fq, norm_prev, precision=hi)
    student = numer / denom[..., None]
    grad_out = 2.0 / length * (student - teacher_out.astype(jnp.float32))
    dnumer = grad_out / denom[..., None]
    ddenom = -jnp.sum(grad_out * student, axis=-1) / denom
    adjoint_local = jnp.einsum("tcf,tcd->cfd", fq, dnumer, precision=hi)
    weight_local = jnp.einsum("tcf,tc->cf", fq, ddenom, precision=hi)
    adjoint_later, weight_later = pick_rows(
        False,
        (
            lax.all_gather(adjoint_local[None], "seq", axis=0, tiled=True),
            lax.all_gather(weight_local[None], "seq", axis=0, tiled=True),
        ),
    )
    dattn = (
        jnp.einsum("tcd,scd->cts", dnumer, vhead, precision=hi) + ddenom.T[:, :, None]
    ) * lower[None]
    dfq = (
        jnp.einsum("cts,scf->tcf", dattn, fk, precision=hi)
        + jnp.einsum("cfd,tcd->tcf", state_prev, dnumer, precision=hi)
        + norm_prev[None] * ddenom[..., None]
    )
    dfk = (
        jnp.einsum("cts,tcf->scf", dattn, fq, precision=hi)
        + jnp.einsum("cfd,scd->scf", adjoint_later, vhead, precision=hi)
        + weight_later[None]
    )
    dq_logits = feature_back(fq, dfq, width)
    dk_logits = feature_back(fk, dfk, width)
    grad_q = jnp.einsum("tcd,tcf->cdf", qfloat, dq_logits, precision=hi)
    grad_k = jnp.einsum("tcd,tcf->cdf", khead, dk_logits, precision=hi)
    reduced = (
        lax.psum_scatter(grad_q, "seq", scatter_dimension=0, tiled=True),
        lax.psum_scatter(grad_k, "seq", scatter_dimension=0, tiled=True),
    )
    return (reduced[0], reduced[1])


def solution(mesh):
    return jax.shard_map(
        shards,
        mesh=mesh,
        in_specs=(
            P("seq", "kv"),
            P("seq", "kv"),
            P("seq", "kv"),
            P("kv", None, None),
            P("kv", None, None),
        ),
        out_specs=(P(("kv", "seq"), None, None), P(("kv", "seq"), None, None)),
        check_vma=False,
    )
```

profile of v0, /device:TPU:0, one launch (start us, length us, event | category | flops | bytes accessed | tf_op | source)
XLA Modules:
  0.0 547.5 jit_solution(18048935345446354479)
XLA Ops:
  7.2 0.7 all-gather.9.cloned.1.call-update
  8.0 0.7 all-gather.11.cloned.1.call-update
  8.7 0.0 all-gather.13.cloned.1.call-start
  8.7 0.9 reshape.123
  9.7 0.8 convolution_bitcast_fusion.1
  10.5 6.9 %fusion.41 = f32[32,256,64]{1,2,0:T(8,128)S(1)} fusion(f32[32,128,64]{1,2,0:T(8,128)S(1)} %copy-done, f32[256,32,128]{2,1,0:T(8,128)S(1)} %convolution_bitcast_fusion.1), kind=kOutput, calls=%fused_computation.58 | convolution fusion | flops 805306368 | bytes 7340032 | tf_op jit(solution)/shard_map/tcd,cdf->tcf/dot_general | solution.py:102
  17.3 1.9 fusion.114
  19.2 1.7 fusion.115
  21.0 2.3 fusion.55
  23.4 3.3 fusion.112
  26.7 0.8 convolution_bitcast_fusion
  27.5 3.0 fusion.113
  30.5 0.6 broadcast_divide_fusion
  31.1 0.9 copy-done.22
  32.1 1.8 broadcast_divide_fusion.2
  33.9 1.4 copy-done.12
  35.2 7.6 %fusion.49 = f32[32,128,128]{2,1,0:T(8,128)} fusion(f32[256,32,128]{2,1,0:T(8,128)S(1)} %convolution_bitcast_fusion, f32[256,32,64]{0,2,1:T(8,128)S(1)} %get-tuple-element.294, f32[256,32,64]{0,2,1:T(8,128)S(1)} %get-tuple-element.295), kind=kOutput, calls=%fused_computation.66 | convolution fusion | flops 1611661312 | bytes 10485760 | tf_op jit(solution)/shard_map/tcf,tcd->cfd/dot_general | solution.py:104
  42.9 0.0 all-gather.15.cloned.1.call-start
  42.9 4.1 copy.88
  47.1 4.0 copy.90
  51.1 3.0 fusion.75
  54.1 34.4 %all-gather.1 = f32[256,128]{1,0:T(8,128)S(1)} all-gather(f32[32,128]{1,0:T(8,128)S(1)} %fusion.75), channel_id=3, replica_groups=mesh['kv'=4,'seq'=8] {'seq'}, dimensions={0}, use_global_device_ids=true | all-gather | bytes 147456 | tf_op jit(solution)/shard_map/all_gather | solution.py:124
  88.5 0.1 multiply_reduce_fusion.9
  88.6 2.1 fusion.96
  90.7 8.0 %multiply_reduce_fusion.2 = (f32[32,256]{1,0:T(8,128)S(1)}, f32[32,256,256]{1,2,0:T(8,128)S(1)}) fusion(f32[256,256]{0,1:T(8,128)S(1)} %fusion.97, f32[256,32,64]{0,2,1:T(8,128)S(1)} %copy-done.9, f32[256,32,64]{0,2,1:T(8,128)S(1)} %copy-done.13, f32[256,32,64]{0,2,1:T(8,128)S(1)} %get-tuple-element.293, f32[256,32,64]{0,2,1:T(8,128)S(1)} %copy-done.2), kind=kOutput, calls=%fused_computation.34 | convolution fusion | flops 3227508736 | bytes 17072128 | tf_op jit(solution)/shard_map/tcf,scf->cts/dot_general | solution.py:127
  98.8 12.4 %fusion.27 = f32[32,128,256]{2,1,0:T(8,128)} fusion(f32[32,256,256]{1,2,0:T(8,128)S(1)} %get-tuple-element.292, f32[256,256]{0,1:T(8,128)S(1)} %fusion.97, f32[256,32,128]{2,1,0:T(8,128)S(1)} %copy-done.6), kind=kOutput, calls=%fused_computation.35 | convolution fusion | flops 3223322624 | bytes 17039360 | tf_op jit(solution)/shard_map/cts,scd->tcd/dot_general | solution.py:128
  111.2 2.2 reshape.125
  113.3 2.4 copy.89
  115.7 2.2 reshape.127
  117.9 2.3 copy.91
  120.2 2.4 broadcast_in_dim.41
  122.7 41.1 %while.18 = (s32[]{:T(128)}, f32[2,16,256]{2,1,0:T(8,128)S(1)}, f32[2,16,256]{2,1,0:T(8,128)S(1)}, f32[2,16,256,128]{3,2,1,0:T(8,128)}, s32[]{:T(128)}, /*index=...) while((s32[]{:T(128)}, f32[2,16,256]{2,1,0:T(8,128)S(1)}, ...), condition=%wide.region_17.18_spmd.clone, body=%wide.region_12.17_spmd.clone.sunk | while | flops 7560381440 | bytes 62398792 | solution.py:75
  123.1 40.5 %conditional.3 = ((f32[2,16,256]{2,1,0:T(8,128)S(1)}, f32[2,16,256]{2,1,0:T(8,128)S(1)}, f32[2,16,256,128]{3,2,1,0:T(8,128)})) conditional(s32[]{:T(128)} %convert_element_type.75, (f32[2,16,256]{2,1,0:T(8,128)S(1)}, f32[2,16,256]{2,1,0:T(8,128)S(1)}, f32[2,16,256,128]{3,2,1,0:T(8,128)}) %tuple.61, (s32[]{:T(128)}, s32[]{:T(128)}, s32[]{:T(128)}, ...), branch_computations={%region_13.13_spmd, %region_14.16_spmd} | conditional | flops 7560381440 | bytes 62397524 | solution.py:68
  123.1 0.1 broadcast_compare_fusion
  123.3 9.9 %fusion.2 = (f32[2,16,256]{2,1,0:T(8,128)S(1)}, f32[2,512,256,16]{2,1,3,0:T(8,128)}) fusion(pred[256,512]{0,1:T(8,128)(4,1)S(1)} %broadcast_compare_fusion, bf16[256,2,16,128]{3,0,2,1:T(8,128)(2,1)} %get-tuple-element.178, bf16[4,512,2,128]{3,1,2,0:T(8,128)(2,1)} %get-tuple-element.176, s32[]{:T(128)S(6)} %select_n.17), kind=kOutput, calls=%fused_computation.3 | convolution fusion | flops 1086316544 | bytes 19300356 | tf_op jit(solution)/shard_map/while/body/eval_jaxpr/cond/branch_1_fun/tgjd,sgd->gjts/dot_general | solution.py:45
  133.2 9.4 %fusion.7 = f32[2,16,256]{2,1,0:T(8,128)S(1)} fusion(f32[2,512,256,16]{2,1,3,0:T(8,128)} %get-tuple-element.280, f32[2,16,256]{2,1,0:T(8,128)S(1)} %max.2, pred[256,512]{0,1:T(8,128)(4,1)S(1)} %broadcast_compare_fusion), kind=kLoop, calls=%fused_computation.7 | loop fusion | flops 16769024 | bytes 16973824 | tf_op jit(solution)/shard_map/while/body/eval_jaxpr/cond/branch_1_fun/reduce_sum | solution.py:53
  142.6 20.9 %multiply_add_fusion = f32[2,16,256,128]{3,2,1,0:T(8,128)} fusion(f32[2,16,256,128]{3,2,1,0:T(8,128)} %get-tuple-element.180, f32[2,16,256]{2,1,0:T(8,128)S(1)} %get-tuple-element.278, f32[2,512,256,16]{2,1,3,0:T(8,128)} %get-tuple-element.280, f32[2,16,256]{2,1,0:T(8,128)S(1)} %max.2, pred[256,512]{0,1:T(8,128)(4,1)S(1)} %broadcast_compare_fusion, ...), kind=kOutput, calls=%fused_computation.12 | convolution fusion | flops 6457131008 | bytes 25624580 | tf_op jit(solution)/shard_map/while/body/eval_jaxpr/cond/branch_1_fun/gjts,sgd->gjtd/dot_general | solution.py:54
  163.8 4.2 convert_bitcast_fusion
  168.0 5.4 copy.92
  173.4 37.9 %all-gather.13.cloned.1.call-done = f32[256,128,128]{2,1,0:T(8,128)} async-done(((f32[32,128,128]{2,1,0:T(8,128)}), f32[256,128,128]{2,1,0:T(8,128)}) %all-gather.13.cloned.1.call-update) | async-done | bytes 16777232 | tf_op jit(solution)/shard_map/all_gather | solution.py:123
  211.3 9.5 %multiply_reduce_fusion.1 = f32[32,128,128]{2,1,0:T(8,128)} fusion(f32[8,32,128,128]{3,2,1,0:T(8,128)} %bitcast.144, f32[8]{0:T(128)S(1)} %compare_convert_fusion.1), kind=kLoop, calls=%fused_computation.32 | loop fusion | flops 7864320 | bytes 18874400 | tf_op jit(solution)/shard_map/reduce_sum | solution.py:116
  220.8 9.5 %multiply_reduce_fusion.3 = (f32[256,32]{0,1:T(8,128)S(1)}, f32[256,32,128]{0,2,1:T(8,128)S(1)}) fusion(f32[256,2,16,128]{0,3,2,1:T(8,128)} %copy.92, f32[256,32]{0,1:T(8,128)S(1)} %fusion.99, f32[32,128,256]{2,1,0:T(8,128)} %fusion.27, f32[32,128,128]{2,1,0:T(8,128)} %multiply_reduce_fusion.1, f32[256,32,64]{0,2,1:T(8,128)S(1)} %get-tuple-element.293, ...), kind=kOutput, calls=%fused_computation.51 | convolution fusion | flops 1618993152 | bytes 18939904 | tf_op jit(solution)/shard_map/tcf,cfd->tcd/dot_general | solution.py:128
  230.3 2.0 copy-done.19
  232.3 5.5 fusion.95
  237.8 0.4 reduce-scatter.3.cloned.1.call-start
  238.3 5.4 fusion.94
  243.6 96.7 %all-gather.3 = f32[256,128]{1,0:T(8,128)S(1)} all-gather(f32[32,128]{1,0:T(8,128)S(1)} %bitcast.151), channel_id=5, replica_groups=mesh['kv'=4,'seq'=8] {'seq'}, dimensions={0}, use_global_device_ids=true | all-gather | bytes 147456 | tf_op jit(solution)/shard_map/all_gather | solution.py:142
  340.4 13.0 %fusion.47 = f32[32,256,256]{1,2,0:T(8,128)S(1)} fusion(f32[256,32,128]{0,2,1:T(8,128)} %copy-done.19, f32[256,32,128]{2,1,0:T(8,128)S(1)} %copy-done.7), kind=kOutput, calls=%fused_computation.64 | convolution fusion | flops 3221225472 | bytes 16777216 | tf_op jit(solution)/shard_map/tcd,scd->cts/dot_general | solution.py:146
  353.4 7.4 %fusion.30 = f32[32,128,256]{2,1,0:T(8,128)} fusion(f32[32,256,256]{1,2,0:T(8,128)S(1)} %fusion.47, f32[32,256]{1,0:T(8,128)S(1)} %bitcast_divide_fusion.1, f32[256,256]{0,1:T(8,128)S(1)} %fusion.97, f32[256,32,64]{0,2,1:T(8,128)S(1)} %copy-done.10, f32[256,32,64]{0,2,1:T(8,128)S(1)} %copy-done.14), kind=kOutput, calls=%fused_computation.38 | convolution fusion | flops 3226468352 | bytes 17072128 | tf_op jit(solution)/shard_map/cts,scf->tcf/dot_general | solution.py:149
  360.8 9.1 %fusion.32 = f32[256,32,128]{0,2,1:T(8,128)S(1)} fusion(f32[32,128,256]{2,1,0:T(8,128)} %fusion.30, f32[256,32,128]{0,2,1:T(8,128)} %copy-done.19, f32[32,128,128]{2,1,0:T(8,128)} %multiply_reduce_fusion.1, f32[256,32]{0,1:T(8,128)S(1)} %negate_divide_fusion, f32[32,128]{1,0:T(8,128)S(1)} %multiply_reduce_fusion.9), kind=kOutput, calls=%fused_computation.44 | convolution fusion | flops 1613758464 | bytes 14729216 | tf_op jit(solution)/shard_map/cfd,tcd->tcf/dot_general | solution.py:150
  370.0 1.2 multiply_reduce_fusion.7
  371.1 0.5 copy-done.21
  371.7 2.9 fusion.85
  374.6 15.4 %fusion.29 = f32[32,128,256]{2,1,0:T(8,128)} fusion(f32[32,256,256]{1,2,0:T(8,128)} %copy-done.16, f32[32,256]{1,0:T(8,128)S(1)} %bitcast_divide_fusion.1, f32[256,256]{0,1:T(8,128)S(1)} %fusion.97, f32[256,32,64]{0,2,1:T(8,128)S(1)} %get-tuple-element.293, f32[256,32,64]{0,2,1:T(8,128)} %get-tuple-element.296), kind=kOutput, calls=%fused_computation.37 | convolution fusion | flops 3226468352 | bytes 17072128 | tf_op jit(solution)/shard_map/cts,tcf->scf/dot_general | solution.py:154
  390.0 0.0 reduce-scatter.5.cloned.1.call-start
  390.0 0.1 multiply_reduce_fusion.8
  390.1 82.9 %all-gather.15.cloned.1.call-done = f32[256,128,128]{2,1,0:T(8,128)} async-done(((f32[32,128,128]{2,1,0:T(8,128)}), f32[256,128,128]{2,1,0:T(8,128)}) %all-gather.15.cloned.1.call-update) | async-done | bytes 16777232 | tf_op jit(solution)/shard_map/all_gather | solution.py:141
  473.0 8.2 %multiply_reduce_fusion = f32[32,128,128]{2,1,0:T(8,128)S(1)} fusion(f32[8,32,128,128]{3,2,1,0:T(8,128)} %bitcast.145, f32[8]{0:T(128)S(1)} %compare_convert_fusion), kind=kLoop, calls=%fused_computation.31 | loop fusion | flops 7864320 | bytes 18874400 | tf_op jit(solution)/shard_map/reduce_sum | solution.py:116
  481.2 10.6 %fusion.31 = f32[256,32,128]{0,2,1:T(8,128)S(1)} fusion(f32[32,128,256]{2,1,0:T(8,128)} %fusion.29, f32[32,128,128]{2,1,0:T(8,128)S(1)} %multiply_reduce_fusion, f32[256,32,128]{2,1,0:T(8,128)} %copy-done.5, f32[32,128]{1,0:T(8,128)S(1)} %multiply_reduce_fusion.8), kind=kOutput, calls=%fused_computation.42 | convolution fusion | flops 1612709888 | bytes 14696448 | tf_op jit(solution)/shard_map/cfd,scd->scf/dot_general | solution.py:155
  491.8 1.2 multiply_reduce_fusion.5
  493.1 1.0 copy-done.18
  494.1 6.9 %fusion.39 = f32[32,128,64]{1,2,0:T(8,128)} fusion(f32[256,32,128]{2,1,0:T(8,128)S(1)} %copy-done.18, f32[256,32,64]{0,2,1:T(8,128)S(1)} %copy-done.11, f32[256,32,64]{0,2,1:T(8,128)S(1)} %copy-done.15, f32[256,32,128]{0,2,1:T(8,128)S(1)} %fusion.31, f32[256,32]{0,1:T(8,128)S(1)} %get-tuple-element.256, f32[256,32]{0,1:T(8,128)S(1)} %get-tuple-element.255), kind=kOutput, calls=%fused_computation.56 | convolution fusion | flops 807927808 | bytes 13697024 | tf_op jit(solution)/shard_map/tcd,tcf->cdf/dot_general | solution.py:161
  501.0 5.7 %reduce-scatter.3.cloned.1.call-done = f32[4,128,64]{1,2,0:T(8,128)} async-done(((f32[32,128,64]{1,2,0:T(8,128)}), f32[4,128,64]{1,2,0:T(8,128)}) %reduce-scatter.3.cloned.1.call-update) | async-done | bytes 131088 | tf_op jit(solution)/shard_map/reduce_scatter | solution.py:163
  506.7 33.6 %reduce-scatter.5.cloned.1.call-done = f32[4,128,64]{1,2,0:T(8,128)} async-done(((f32[32,128,64]{1,2,0:T(8,128)}), f32[4,128,64]{1,2,0:T(8,128)}) %reduce-scatter.5.cloned.1.call-update) | async-done | bytes 131088 | tf_op jit(solution)/shard_map/reduce_scatter | solution.py:164
  (77 shorter events, 0.4 us)
Async XLA Ops:
  7.2 3.3 copy-start
  7.2 104.0 %all-gather.9.cloned.1.call-start = ((), (), s32[]{:S(2)}) async-start(), calls=%async_computation.2 | async-start | bytes 1179648 | tf_op jit(solution)/shard_map/all_gather | solution.py:86
  7.9 107.8 %all-gather.11.cloned.1.call-start = ((), (), s32[]{:S(2)}) async-start(), calls=%async_computation.3 | async-start | bytes 1179648 | tf_op jit(solution)/shard_map/all_gather | solution.py:87
  8.7 202.7 %all-gather.13.cloned.1.call-start = ((), (), s32[]{:S(2)}) async-start(), calls=%async_computation.6 | async-start | bytes 18874368 | tf_op jit(solution)/shard_map/all_gather | solution.py:123
  10.4 8.8 %copy-start.17 = (f32[256,32,128]{2,1,0:T(8,128)}, f32[256,32,128]{2,1,0:T(8,128)S(1)}, u32[]{:S(2)}) copy-start(f32[256,32,128]{2,1,0:T(8,128)S(1)} %convolution_bitcast_fusion.1) | copy-start | bytes 12582916
  17.3 3.7 copy-start.25
  17.3 3.7 copy-start.20
  17.3 3.7 copy-start.24
  26.7 3.8 copy-start.23
  27.5 6.4 %copy-start.5 = (f32[256,32,128]{2,1,0:T(8,128)}, f32[256,32,128]{2,1,0:T(8,128)S(1)}, u32[]{:S(2)}) copy-start(f32[256,32,128]{2,1,0:T(8,128)S(1)} %convolution_bitcast_fusion) | copy-start | bytes 12582916
  30.5 1.6 copy-start.22
  31.1 2.8 copy-start.8
  33.9 1.4 copy-start.12
  42.9 430.1 %all-gather.15.cloned.1.call-start = ((), (), s32[]{:S(2)}) async-start(), calls=%async_computation.7 | async-start | bytes 18874368 | tf_op jit(solution)/shard_map/all_gather | solution.py:141
  51.1 37.5 %copy-start.2 = (f32[256,32,64]{0,2,1:T(8,128)S(1)}, f32[256,32,64]{0,2,1:T(8,128)}, u32[]{:S(2)}) copy-start(f32[256,32,64]{0,2,1:T(8,128)} %get-tuple-element.296) | copy-start | bytes 6291460
  51.1 39.6 %copy-start.9 = (f32[256,32,64]{0,2,1:T(8,128)S(1)}, f32[256,32,64]{0,2,1:T(8,128)}, u32[]{:S(2)}) copy-start(f32[256,32,64]{0,2,1:T(8,128)} %copy-done.8) | copy-start | bytes 6291460
  51.1 39.6 %copy-start.13 = (f32[256,32,64]{0,2,1:T(8,128)S(1)}, f32[256,32,64]{0,2,1:T(8,128)}, u32[]{:S(2)}) copy-start(f32[256,32,64]{0,2,1:T(8,128)} %copy-done.12) | copy-start | bytes 6291460
  90.7 8.0 %copy-start.6 = (f32[256,32,128]{2,1,0:T(8,128)S(1)}, f32[256,32,128]{2,1,0:T(8,128)}, u32[]{:S(2)}) copy-start(f32[256,32,128]{2,1,0:T(8,128)} %copy-done.5) | copy-start | bytes 12582916
  220.8 11.5 %copy-start.3 = (f32[256,32,64]{0,2,1:T(8,128)S(1)}, f32[256,32,64]{0,2,1:T(8,128)}, u32[]{:S(2)}) copy-start(f32[256,32,64]{0,2,1:T(8,128)} %get-tuple-element.296) | copy-start | bytes 6291460
  230.3 2.0 copy-start.19
  237.8 268.9 %reduce-scatter.3.cloned.1.call-start = ((), (), s32[]{:S(2)}) async-start(), calls=%async_computation.4 | async-start | bytes 1179648 | tf_op jit(solution)/shard_map/reduce_scatter | solution.py:163
  238.2 102.1 %copy-start.7 = (f32[256,32,128]{2,1,0:T(8,128)S(1)}, f32[256,32,128]{2,1,0:T(8,128)}, u32[]{:S(2)}) copy-start(f32[256,32,128]{2,1,0:T(8,128)} %copy-done.5) | copy-start | bytes 12582916
  340.4 13.0 %copy-start.10 = (f32[256,32,64]{0,2,1:T(8,128)S(1)}, f32[256,32,64]{0,2,1:T(8,128)}, u32[]{:S(2)}) copy-start(f32[256,32,64]{0,2,1:T(8,128)} %copy-done.8) | copy-start | bytes 6291460
  340.4 13.0 %copy-start.14 = (f32[256,32,64]{0,2,1:T(8,128)S(1)}, f32[256,32,64]{0,2,1:T(8,128)}, u32[]{:S(2)}) copy-start(f32[256,32,64]{0,2,1:T(8,128)} %copy-done.12) | copy-start | bytes 6291460
  353.4 7.4 %copy-start.16 = (f32[32,256,256]{1,2,0:T(8,128)}, f32[32,256,256]{1,2,0:T(8,128)S(1)}, u32[]{:S(2)}) copy-start(f32[32,256,256]{1,2,0:T(8,128)S(1)} %fusion.47) | copy-start | bytes 25165828
  360.8 9.1 %copy-start.4 = (f32[256,32,64]{0,2,1:T(8,128)S(1)}, f32[256,32,64]{0,2,1:T(8,128)}, u32[]{:S(2)}) copy-start(f32[256,32,64]{0,2,1:T(8,128)} %get-tuple-element.296) | copy-start | bytes 6291460
  370.0 1.7 copy-start.21
  390.0 150.3 %reduce-scatter.5.cloned.1.call-start = ((), (), s32[]{:S(2)}) async-start(), calls=%async_computation.5 | async-start | bytes 1179648 | tf_op jit(solution)/shard_map/reduce_scatter | solution.py:164
  481.2 10.6 %copy-start.11 = (f32[256,32,64]{0,2,1:T(8,128)S(1)}, f32[256,32,64]{0,2,1:T(8,128)}, u32[]{:S(2)}) copy-start(f32[256,32,64]{0,2,1:T(8,128)} %copy-done.8) | copy-start | bytes 6291460
  481.2 10.6 %copy-start.15 = (f32[256,32,64]{0,2,1:T(8,128)S(1)}, f32[256,32,64]{0,2,1:T(8,128)}, u32[]{:S(2)}) copy-start(f32[256,32,64]{0,2,1:T(8,128)} %copy-done.12) | copy-start | bytes 6291460
  491.8 2.2 copy-start.18
  493.0 47.2 %copy-start.1 = (f32[32,128,64]{1,2,0:T(8,128)S(1)}, f32[32,128,64]{1,2,0:T(8,128)}, u32[]{:S(2)}) copy-start(f32[32,128,64]{1,2,0:T(8,128)} %param.13) | copy-start | bytes 3145732
Sparse Core Ops, SparseCore 0:
  9.6 24.9 all-gather.8
  36.2 21.9 all-gather.10
  59.8 151.5 all-gather.12
  237.9 235.0 all-gather.14
  475.7 30.9 reduce-scatter.2
  509.4 30.8 reduce-scatter.4
where the time goes:
time: 555 us; the launch traced here: 548 us
  waiting for transfers between devices  161 us (29%)
  matrix products  157 us (28%)
  blocking collectives  131 us (24%)
  other arithmetic  49.4 us (9%)
  local copies, waits for them, and re-layouts  31.9 us (6%)
  between operations  15 us (3%)
    all_gather x1, blocking collectives, shards(): lax.all_gather(weight_local[None], 'seq', axis=0, tiled=True)  96.7 us
    all_gather x1, waiting for transfers between devices, shards(): lax.all_gather(adjoint_local[None], 'seq', axis=0, tiled=True)  82.9 us
    all_gather x1, waiting for transfers between devices, shards(): lax.all_gather(state_local[None], 'seq', axis=0, tiled=True)  37.9 us
    all_gather x1, blocking collectives, shards(): lax.all_gather(norm_local[None], 'seq', axis=0, tiled=True)  34.4 us
    reduce_scatter x1, waiting for transfers between devices, shards(): lax.psum_scatter(grad_k, 'seq', scatter_dimension=0, tiled=True)  33.6 us
    dot_general x1, matrix products, teacher_block(): jnp.einsum('gjts,sgd->gjtd', probs, vblock.astype(jnp.float32), precision...  20.9 us
    unnamed x56, local copies, waits for them, and re-layouts  18.7 us
    reduce_sum x2, other arithmetic, pick_rows(): jnp.sum(weight[:, None, None, None] * piece[0], axis=0)  17.7 us
  transfers between devices with their start and end apart: 6, of which 4 were waited for; matrix products, arithmetic and copies ran while one was open for 38% of the time, Pallas kernels for 0%

commit v1 on v0

v1 whole, which is shorter than its diff:
```python
import functools

import jax
import jax.numpy as jnp
from jax import lax
from jax.experimental import pallas as pl
from jax.experimental.pallas import tpu as pltpu
from jax.sharding import PartitionSpec as P

HD = 128
ONES = 16
F32 = jnp.float32
BF16 = jnp.bfloat16
LOG2E = 1.4426950408889634


def nn(a, b):
    return lax.dot_general(a, b, (((1,), (0,)), ((), ())), preferred_element_type=F32)


def nt(a, b):
    return lax.dot_general(a, b, (((1,), (1,)), ((), ())), preferred_element_type=F32)


def split(x):
    high = x.astype(BF16)
    return high, (x - high.astype(F32)).astype(BF16)


def cat(parts, axis):
    return jnp.concatenate(parts, axis=axis)


def feature(logits):
    first = jnp.exp(logits - jnp.max(logits, axis=0, keepdims=True))
    second = jnp.exp(jnp.min(logits, axis=0, keepdims=True) - logits)
    first = first * (1.0 / jnp.sum(first, axis=0, keepdims=True))
    second = second * (1.0 / jnp.sum(second, axis=0, keepdims=True))
    return cat([first, second], 0)


def feature_back(phi, dphi):
    width = phi.shape[0] // 2
    prod = phi * dphi
    one = prod[:width] - phi[:width] * jnp.sum(prod[:width], axis=0, keepdims=True)
    two = prod[width:] - phi[width:] * jnp.sum(prod[width:], axis=0, keepdims=True)
    return one - two


def teacher(c, chunk, q, k_ref, va_ref, lower):
    scale = LOG2E / HD**0.5
    if c < 8:
        scores = [nt(k_ref[j * chunk : (j + 1) * chunk, :], q) for j in range(c + 1)]
        scores[c] = jnp.where(lower, scores[c], -1e30)
        peak = functools.reduce(jnp.maximum, scores)
        peak = jnp.max(peak, axis=0, keepdims=True) * scale
        acc = None
        for j in range(c + 1):
            probs = jnp.exp2(scores[j] * scale - peak).astype(BF16)
            part = nn(va_ref[:, j * chunk : (j + 1) * chunk], probs)
            acc = part if acc is None else acc + part
    else:

        def step(scores, start, state):
            peak, acc = state
            new = jnp.maximum(peak, jnp.max(scores, axis=0, keepdims=True) * scale)
            probs = jnp.exp2(scores * scale - new).astype(BF16)
            part = nn(va_ref[:, pl.ds(start, chunk)], probs)
            return new, acc * jnp.exp2(peak - new) + part

        def body(j, state):
            start = pl.multiple_of(j * chunk, chunk)
            return step(nt(k_ref[pl.ds(start, chunk), :], q), start, state)

        state = (
            jnp.full((1, chunk), -1e30, F32),
            jnp.zeros((HD + ONES, chunk), F32),
        )
        state = lax.fori_loop(0, c, body, state)
        last = jnp.where(lower, nt(k_ref[c * chunk : (c + 1) * chunk, :], q), -1e30)
        acc = step(last, c * chunk, state)[1]
    return (acc[:HD] * (1.0 / acc[HD : HD + 1])).astype(BF16).astype(F32)


def kernel(
    chunk, pos_ref, q_ref, k_ref, v_ref, wq_ref, wk_ref, gq_ref, gk_ref,
    va_ref, fk_ref, dfk_ref, adj_ref, wgt_ref,
):
    length = q_ref.shape[0]
    blocks = length // chunk

    @pl.when(pl.program_id(0) == 0)
    def _():
        va_ref[HD:, :] = jnp.ones((ONES, length), BF16)
        for c in range(blocks):
            cols = slice(c * chunk, (c + 1) * chunk)
            va_ref[:HD, cols] = v_ref[cols, :].astype(F32).T.astype(BF16)

    src = lax.broadcasted_iota(jnp.int32, (chunk, chunk), 0)
    dst = lax.broadcasted_iota(jnp.int32, (chunk, chunk), 1)
    lower = src <= dst
    wq2 = cat(split(wq_ref[0].T), 1)
    wk2 = cat(split(wk_ref[0].T), 1)
    width = wq2.shape[0]
    gq = jnp.zeros((width, HD), F32)
    state = jnp.zeros((HD + ONES, 2 * width), F32)
    norm = jnp.zeros((2 * width, 1), F32)
    for c in range(blocks):
        cols = slice(c * chunk, (c + 1) * chunk)
        q = q_ref[cols, :]
        k = k_ref[cols, :]
        v = v_ref[cols, :]
        va = va_ref[:, cols]
        target = teacher(c, chunk, q, k_ref, va_ref, lower)
        fq = feature(nt(wq2, cat([q, q], 1)))
        fk = feature(nt(wk2, cat([k, k], 1)))
        fk_ref[:, cols] = fk
        fqh, fql = split(fq)
        fkh, fkl = split(fk)
        frh, frl = split(fk.T)
        attn = nn(cat([frh, frl, frh], 1), cat([fqh, fqh, fql], 0))
        ath, atl = split(jnp.where(lower, attn, 0.0))
        sth, stl = split(state)
        num = nn(
            cat([va, va, sth, stl, sth], 1), cat([ath, atl, fqh, fqh, fql], 0)
        )
        inv = 1.0 / num[HD : HD + 1]
        student = num[:HD] * inv
        grad = (2.0 / length) * (student - target)
        dnum = grad * inv
        dden = -jnp.sum(grad * student, axis=0, keepdims=True) * inv
        dnh, dnl = split(dnum)
        dattn = nn(cat([v, v], 1), cat([dnh, dnl], 0)) + dden
        dah, dal = split(jnp.where(lower, dattn, 0.0))
        srh, srl = split(state[:HD].T)
        dfq = nn(
            cat([fkh, fkl, fkh, srh, srl, srh], 1),
            cat([dah, dah, dal, dnh, dnh, dnl], 0),
        ) + norm * dden
        dql = cat(split(feature_back(fq, dfq)), 0)
        both = nn(dql, q)
        gq = gq + both[:width] + both[width:]
        dfk_ref[:, cols] = nt(cat([fqh, fql, fqh], 1), cat([dah, dah, dal], 1))
        adj_ref[c] = nt(cat([fqh, fql, fqh], 1), cat([dnh, dnh, dnl], 1))
        wgt_ref[c] = jnp.broadcast_to(
            jnp.sum(fq * dden, axis=1, keepdims=True), wgt_ref.shape[1:]
        )
        both = nn(va, cat([frh, frl], 1))
        state = state + both[:, : 2 * width] + both[:, 2 * width :]
        norm = norm + jnp.sum(fk, axis=1, keepdims=True)
    gq_ref[0] = gq.T

    gk = jnp.zeros((width, HD), F32)
    adj = jnp.zeros((2 * width, HD), F32)
    wgt = jnp.zeros((2 * width, 1), F32)
    for c in reversed(range(blocks)):
        cols = slice(c * chunk, (c + 1) * chunk)
        v = v_ref[cols, :]
        dfk = dfk_ref[:, cols] + nt(cat(split(adj), 1), cat([v, v], 1)) + wgt
        dkl = cat(split(feature_back(fk_ref[:, cols], dfk)), 0)
        both = nn(dkl, k_ref[cols, :])
        gk = gk + both[:width] + both[width:]
        adj = adj + adj_ref[c]
        wgt = wgt + wgt_ref[c][:, :1]
    gk_ref[0] = gk.T


def shards(devices, queries, keys, values, query_map, key_map):
    tok = queries.shape[0]
    heads_dev = queries.shape[1] // HD
    kv_dev = keys.shape[1] // HD
    group = heads_dev // kv_dev
    own = heads_dev // devices
    width = query_map.shape[2]
    length = tok * devices
    parts = []
    for d in range(devices):
        g = d * own // group
        parts.append(queries[:, d * own * HD : (d + 1) * own * HD])
        parts.append(keys[:, g * HD : (g + 1) * HD])
        parts.append(values[:, g * HD : (g + 1) * HD])
    packed = jnp.stack(
        [cat(parts[3 * d : 3 * d + 3], 1) for d in range(devices)], axis=0
    )
    held = lax.all_to_all(packed, "seq", 0, 0, tiled=True)
    held = held.reshape(length, (own + 2) * HD)
    position = lax.axis_index("seq").astype(jnp.int32).reshape(1)
    chunk = 256 if length % 256 == 0 else HD
    blocks = length // chunk
    weights = pl.BlockSpec((1, HD, width), lambda h, pos: (pos[0] * own + h, 0, 0))
    grads = pl.BlockSpec((1, HD, width), lambda h, pos: (h, 0, 0))
    gq, gk = pl.pallas_call(
        functools.partial(kernel, chunk),
        grid_spec=pltpu.PrefetchScalarGridSpec(
            num_scalar_prefetch=1,
            grid=(own,),
            in_specs=[
                pl.BlockSpec((length, HD), lambda h, pos: (0, h)),
                pl.BlockSpec((length, HD), lambda h, pos: (0, own)),
                pl.BlockSpec((length, HD), lambda h, pos: (0, own + 1)),
                weights,
                weights,
            ],
            out_specs=[grads, grads],
            scratch_shapes=[
                pltpu.VMEM((HD + ONES, length), BF16),
                pltpu.VMEM((2 * width, length), F32),
                pltpu.VMEM((2 * width, length), F32),
                pltpu.VMEM((blocks, 2 * width, HD), F32),
                pltpu.VMEM((blocks, 2 * width, HD), F32),
            ],
        ),
        out_shape=[jax.ShapeDtypeStruct((own, HD, width), F32)] * 2,
        compiler_params=pltpu.CompilerParams(
            dimension_semantics=("arbitrary",), vmem_limit_bytes=60 * 1024 * 1024
        ),
    )(position, held, held, held, query_map, key_map)
    return gq, gk


def solution(mesh):
    return jax.shard_map(
        functools.partial(shards, mesh.shape["seq"]),
        mesh=mesh,
        in_specs=(
            P("seq", "kv"),
            P("seq", "kv"),
            P("seq", "kv"),
            P("kv", None, None),
            P("kv", None, None),
        ),
        out_specs=(P(("kv", "seq"), None, None), P(("kv", "seq"), None, None)),
        check_vma=False,
    )
```

time: 555 us -> 161 us (0.29); the launches traced: 548 us -> 160 us
  matrix products: 157 us -> 0 us
  blocking collectives: 131 us -> 0 us
  waiting for transfers between devices: 161 us -> 65.1 us
  Pallas kernels: 0 us -> 68.7 us
  other arithmetic: 49.4 us -> 6.3 us
  local copies, waits for them, and re-layouts: 31.9 us -> 13.2 us
  between operations: 15 us -> 0.68 us
  starting transfers between devices: 0.64 us -> 6.35 us
    dot_general x20 -> x0, matrix products: 157 us -> none  [the longest x1 20.9 us: teacher_block(): jnp.einsum('gjts,sgd->gjtd', probs, vblock.astype(jnp.float32), precision...]
    all_gather x2 -> x0, blocking collectives: 131 us -> none  [the longest x1 96.7 us: shards(): lax.all_gather(weight_local[None], 'seq', axis=0, tiled=True)]
    all_gather x4 -> x0, waiting for transfers between devices: 121 us -> none  [the longest x1 82.9 us: shards(): lax.all_gather(adjoint_local[None], 'seq', axis=0, tiled=True)]
    pallas_call x0 -> x1, Pallas kernels: none -> 68.7 us  [shards(): pl.pallas_call(functools.partial(kernel, chunk), grid_spec=pltpu.Prefetch...]
    all_to_all x0 -> x1, waiting for transfers between devices: none -> 65.1 us  [shards(): held = lax.all_to_all(packed, 'seq', 0, 0, tiled=True)]
    reduce_scatter x2 -> x0, waiting for transfers between devices: 39.2 us -> none  [the longest x1 33.6 us: shards(): lax.psum_scatter(grad_k, 'seq', scatter_dimension=0, tiled=True)]
    reduce_sum x8 -> x0, other arithmetic: 32.6 us -> none  [the longest x2 17.7 us: pick_rows(): jnp.sum(weight[:, None, None, None] * piece[0], axis=0)]
    unnamed x56 -> x8, local copies, waits for them, and re-layouts: 18.7 us -> 8.03 us
  transfers between devices with their start and end apart: 6 -> 1, of which waited for: 4 -> 1; matrix products, arithmetic and copies ran while one was open for 38% -> 4% of each run, Pallas kernels for 0% -> 0%
where the time goes in v1:
time: 161 us; the launch traced here: 160 us
  Pallas kernels  68.7 us (43%)
  waiting for transfers between devices  65.1 us (40%)
  local copies, waits for them, and re-layouts  13.2 us (8%)
  starting transfers between devices  6.35 us (4%)
  other arithmetic  6.3 us (4%)
    pallas_call x1, Pallas kernels, shards(): pl.pallas_call(functools.partial(kernel, chunk), grid_spec=pltpu.Prefetch...  68.7 us
    all_to_all x1, waiting for transfers between devices, shards(): held = lax.all_to_all(packed, 'seq', 0, 0, tiled=True)  65.1 us
    unnamed x8, local copies, waits for them, and re-layouts  8.03 us
    all_to_all x1, starting transfers between devices, shards(): held = lax.all_to_all(packed, 'seq', 0, 0, tiled=True)  6.35 us
    unnamed x7, other arithmetic  5.51 us
    pallas_call x2, local copies, waits for them, and re-layouts, shards(): pl.pallas_call(functools.partial(kernel, chunk), grid_spec=pltpu.Prefetch...  3.44 us
  transfers between devices with their start and end apart: 1, of which 1 were waited for; matrix products, arithmetic and copies ran while one was open for 4% of the time, Pallas kernels for 0%

profile of v1, /device:TPU:0, one launch (start us, length us, event | category | flops | bytes accessed | tf_op | source)
XLA Modules:
  0.0 160.4 jit_solution(4309256766418091267)
XLA Ops:
  0.6 0.0 copy-start.1
  0.6 0.0 copy-start.2
  0.6 1.7 %fusion.16 = (bf16[256,512]{1,0:T(8,128)(2,1)S(1)}, bf16[256,512]{1,0:T(8,128)(2,1)S(1)}, bf16[256,512]{1,0:T(8,128)(2,1)S(1)}, bf16[256,512]{1,0:T(8,128)(2,1)S...) fusion(bf16[256,4096]{1,0:T(8,128)(2,1)} %param.5), kind=kLoop, calls=%fused_computation.32 | loop fusion | bytes 4194304 | tf_op jit(solution)/shard_map/slice | solution.py:179
  2.4 0.0 copy-done.1
  2.4 0.0 copy-done.2
  2.4 0.8 fusion.9
  3.2 0.8 fusion.11
  4.0 0.8 fusion.13
  4.8 0.8 fusion.15
  5.6 0.8 fusion.1
  6.4 0.8 fusion.3
  7.2 0.8 fusion.5
  7.9 0.8 fusion.7
  8.7 6.4 %all-to-all-start = ((bf16[8,256,768]{2,1,0:T(8,128)(2,1)}), bf16[8,256,768]{2,1,0:T(8,128)(2,1)S(1)}, u32[]{:S(2)}, u32[]{:S(2)}) async-start(bf16[8,256,768]{2,1,0:T(8,128)(2,1)} %fusion.7), calls=%async_computation | async-start | bytes 6291456 | tf_op jit(solution)/shard_map/all_to_all | solution.py:185
  15.1 3.2 %copy.7.wq_ref = f32[32,128,64]{2,1,0:T(8,128)} copy(f32[32,128,64]{1,2,0:T(8,128)} %param.8) | data formatting | bytes 2097152 | tf_op args[3]
  18.3 3.2 %copy.8.wk_ref = f32[32,128,64]{2,1,0:T(8,128)} copy(f32[32,128,64]{1,2,0:T(8,128)} %param.9) | data formatting | bytes 2097152 | tf_op args[4]
  21.5 65.1 %all-to-all-done = bf16[8,256,768]{2,1,0:T(8,128)(2,1)S(1)} async-done(((bf16[8,256,768]{2,1,0:T(8,128)(2,1)}), bf16[8,256,768]{2,1,0:T(8,128)(2,1)S(1)}, u32[]{:S(2)}, u32[]{:S(2)}) %all-to-all-start) | async-done | bytes 3145760 | tf_op jit(solution)/shard_map/all_to_all | solution.py:185
  86.6 0.0 copy-start
  86.6 1.6 %copy-done = bf16[8,256,768]{2,1,0:T(8,128)(2,1)} copy-done((bf16[8,256,768]{2,1,0:T(8,128)(2,1)}, bf16[8,256,768]{2,1,0:T(8,128)(2,1)S(1)}, u32[]{:S(2)}) %copy-start) | copy-done | bytes 3145752
  88.2 68.7 %shard_map.68 = (f32[4,128,64]{2,1,0:T(8,128)}, f32[4,128,64]{2,1,0:T(8,128)}) custom-call(s32[1]{0:T(128)} %bitcast.pos_ref, bf16[2048,768]{1,0:T(8,128)(2,1)} %bitcast.34, bf16[2048,768]{1,0:T(8,128)(2,1)} %bitcast.35, bf16[2048,768]{1,0:T(8,128)(2,1)} %bitcast.36, f32[32,128,64]{2,1,0:T(8,128)} %copy.7.wq_ref, f32[32,128,64]{2,1,0:T(8,128)} %copy.8.wk_ref), custom_call_target="tpu_custom_call" | custom-call | tf_op jit(solution)/shard_map/pallas_call | solution.py:192
  156.9 1.7 %copy.10 = f32[4,128,64]{1,2,0:T(8,128)} copy(f32[4,128,64]{2,1,0:T(8,128)} %get-tuple-element.3) | data formatting | bytes 262144 | tf_op jit(solution)/shard_map/pallas_call | solution.py:192
  158.6 1.7 %copy.9 = f32[4,128,64]{1,2,0:T(8,128)} copy(f32[4,128,64]{2,1,0:T(8,128)} %get-tuple-element.2) | data formatting | bytes 262144 | tf_op jit(solution)/shard_map/pallas_call | solution.py:192
  (1 shorter events, 0.0 us)
Async XLA Ops:
  0.6 1.7 %copy-start.1 = (bf16[256,256]{1,0:T(8,128)(2,1)S(1)}, bf16[256,256]{1,0:T(8,128)(2,1)}, u32[]{:S(2)}) copy-start(bf16[256,256]{1,0:T(8,128)(2,1)} %param.6) | copy-start | bytes 393220
  0.6 1.7 %copy-start.2 = (bf16[256,256]{1,0:T(8,128)(2,1)S(1)}, bf16[256,256]{1,0:T(8,128)(2,1)}, u32[]{:S(2)}) copy-start(bf16[256,256]{1,0:T(8,128)(2,1)} %param.7) | copy-start | bytes 393220
  8.7 77.9 %all-to-all-start = ((bf16[8,256,768]{2,1,0:T(8,128)(2,1)}), bf16[8,256,768]{2,1,0:T(8,128)(2,1)S(1)}, u32[]{:S(2)}, u32[]{:S(2)}) async-start(bf16[8,256,768]{2,1,0:T(8,128)(2,1)} %fusion.7), calls=%async_computation | async-start | bytes 6291456 | tf_op jit(solution)/shard_map/all_to_all | solution.py:185
  86.6 1.6 %copy-start = (bf16[8,256,768]{2,1,0:T(8,128)(2,1)}, bf16[8,256,768]{2,1,0:T(8,128)(2,1)S(1)}, u32[]{:S(2)}) copy-start(bf16[8,256,768]{2,1,0:T(8,128)(2,1)S(1)} %all-to-all-done) | copy-start | bytes 9437188

commit v2 on v1

--- a/solution.py
+++ b/solution.py
@@ -99,8 +99,8 @@
     src = lax.broadcasted_iota(jnp.int32, (chunk, chunk), 0)
     dst = lax.broadcasted_iota(jnp.int32, (chunk, chunk), 1)
     lower = src <= dst
-    wq2 = cat(split(wq_ref[0].T), 1)
-    wk2 = cat(split(wk_ref[0].T), 1)
+    wq2 = cat(split(wq_ref[0]), 1)
+    wk2 = cat(split(wk_ref[0]), 1)
     width = wq2.shape[0]
     gq = jnp.zeros((width, HD), F32)
     state = jnp.zeros((HD + ONES, 2 * width), F32)
@@ -148,7 +148,7 @@
         both = nn(va, cat([frh, frl], 1))
         state = state + both[:, : 2 * width] + both[:, 2 * width :]
         norm = norm + jnp.sum(fk, axis=1, keepdims=True)
-    gq_ref[0] = gq.T
+    gq_ref[0] = gq
 
     gk = jnp.zeros((width, HD), F32)
     adj = jnp.zeros((2 * width, HD), F32)
@@ -162,7 +162,7 @@
         gk = gk + both[:width] + both[width:]
         adj = adj + adj_ref[c]
         wgt = wgt + wgt_ref[c][:, :1]
-    gk_ref[0] = gk.T
+    gk_ref[0] = gk
 
 
 def shards(devices, queries, keys, values, query_map, key_map):
@@ -173,49 +173,76 @@
     own = heads_dev // devices
     width = query_map.shape[2]
     length = tok * devices
-    parts = []
-    for d in range(devices):
-        g = d * own // group
-        parts.append(queries[:, d * own * HD : (d + 1) * own * HD])
-        parts.append(keys[:, g * HD : (g + 1) * HD])
-        parts.append(values[:, g * HD : (g + 1) * HD])
-    packed = jnp.stack(
-        [cat(parts[3 * d : 3 * d + 3], 1) for d in range(devices)], axis=0
-    )
-    held = lax.all_to_all(packed, "seq", 0, 0, tiled=True)
-    held = held.reshape(length, (own + 2) * HD)
     position = lax.axis_index("seq").astype(jnp.int32).reshape(1)
     chunk = 256 if length % 256 == 0 else HD
     blocks = length // chunk
-    weights = pl.BlockSpec((1, HD, width), lambda h, pos: (pos[0] * own + h, 0, 0))
-    grads = pl.BlockSpec((1, HD, width), lambda h, pos: (h, 0, 0))
-    gq, gk = pl.pallas_call(
-        functools.partial(kernel, chunk),
-        grid_spec=pltpu.PrefetchScalarGridSpec(
-            num_scalar_prefetch=1,
-            grid=(own,),
+    maps = (jnp.swapaxes(query_map, 1, 2), jnp.swapaxes(key_map, 1, 2))
+
+    def pack(first, count, extra):
+        def body(*refs):
+            for i, ref in enumerate(refs[:-1]):
+                start = count * HD + (i - 1) * HD if i else 0
+                refs[-1][0, :, start : start + ref.shape[1]] = ref[...]
+
+        columns = (count + len(extra)) * HD
+        return pl.pallas_call(
+            body,
+            grid=(devices,),
             in_specs=[
-                pl.BlockSpec((length, HD), lambda h, pos: (0, h)),
-                pl.BlockSpec((length, HD), lambda h, pos: (0, own)),
-                pl.BlockSpec((length, HD), lambda h, pos: (0, own + 1)),
-                weights,
-                weights,
-            ],
-            out_specs=[grads, grads],
-            scratch_shapes=[
-                pltpu.VMEM((HD + ONES, length), BF16),
-                pltpu.VMEM((2 * width, length), F32),
-                pltpu.VMEM((2 * width, length), F32),
-                pltpu.VMEM((blocks, 2 * width, HD), F32),
-                pltpu.VMEM((blocks, 2 * width, HD), F32),
-            ],
-        ),
-        out_shape=[jax.ShapeDtypeStruct((own, HD, width), F32)] * 2,
-        compiler_params=pltpu.CompilerParams(
-            dimension_semantics=("arbitrary",), vmem_limit_bytes=60 * 1024 * 1024
-        ),
-    )(position, held, held, held, query_map, key_map)
-    return gq, gk
+                pl.BlockSpec(
+                    (tok, count * HD), lambda d: (0, (d * own + first) // count)
+                )
+            ]
+            + [pl.BlockSpec((tok, HD), lambda d: (0, d * own // group))] * len(extra),
+            out_specs=pl.BlockSpec((1, tok, columns), lambda d: (d, 0, 0)),
+            out_shape=jax.ShapeDtypeStruct((devices, tok, columns), BF16),
+        )(queries, *extra)
+
+    def send(packed):
+        held = lax.all_to_all(packed, "seq", 0, 0, tiled=True)
+        return held.reshape(length, packed.shape[2])
+
+    def run(first, count, held, shared, base):
+        weights = pl.BlockSpec(
+            (1, width, HD), lambda h, pos: (pos[0] * own + first + h, 0, 0)
+        )
+        grads = pl.BlockSpec((1, width, HD), lambda h, pos: (h, 0, 0))
+        return pl.pallas_call(
+            functools.partial(kernel, chunk),
+            grid_spec=pltpu.PrefetchScalarGridSpec(
+                num_scalar_prefetch=1,
+                grid=(count,),
+                in_specs=[
+                    pl.BlockSpec((length, HD), lambda h, pos: (0, h)),
+                    pl.BlockSpec((length, HD), lambda h, pos: (0, base)),
+                    pl.BlockSpec((length, HD), lambda h, pos: (0, base + 1)),
+                    weights,
+                    weights,
+                ],
+                out_specs=[grads, grads],
+                scratch_shapes=[
+                    pltpu.VMEM((HD + ONES, length), BF16),
+                    pltpu.VMEM((2 * width, length), F32),
+                    pltpu.VMEM((2 * width, length), F32),
+                    pltpu.VMEM((blocks, 2 * width, HD), F32),
+                    pltpu.VMEM((blocks, 2 * width, HD), F32),
+                ],
+            ),
+            out_shape=[jax.ShapeDtypeStruct((count, width, HD), F32)] * 2,
+            compiler_params=pltpu.CompilerParams(
+                dimension_semantics=("arbitrary",),
+                vmem_limit_bytes=40 * 1024 * 1024,
+            ),
+        )(position, held, shared, shared, *maps)
+
+    count = own // 2 if own % 2 == 0 else own
+    shared = send(pack(0, count, (keys, values)))
+    grads = [run(0, count, shared, shared, count)]
+    if count < own:
+        packed, shared = lax.optimization_barrier((pack(count, count, ()), shared))
+        grads.append(run(count, count, send(packed), shared, count))
+    gq, gk = (cat([g[i] for g in grads], 0) for i in range(2))
+    return jnp.swapaxes(gq, 1, 2), jnp.swapaxes(gk, 1, 2)
 
 
 def solution(mesh):

time: 161 us -> 138 us (0.86)
  waiting for transfers between devices: 65.1 us -> 43.7 us
  local copies, waits for them, and re-layouts: 13.2 us -> 2.44 us
  Pallas kernels: 68.7 us -> 78.8 us
  other arithmetic: 6.3 us -> 0.72 us
  starting transfers between devices: 6.35 us -> 10.6 us
    all_to_all x1 -> x2, waiting for transfers between devices: 65.1 us -> 43.7 us  [send(): held = lax.all_to_all(packed, 'seq', 0, 0, tiled=True)]
    pallas_call x1 -> x4, Pallas kernels: 68.7 us -> 78.8 us  [the longest x2 67.9 us: run(): pl.pallas_call(functools.partial(kernel, chunk), grid_spec=pltpu.Prefetch...]
    unnamed x8 -> x6, local copies, waits for them, and re-layouts: 8.03 us -> 2.44 us
    unnamed x7 -> x0, other arithmetic: 5.51 us -> none
    all_to_all x1 -> x2, starting transfers between devices: 6.35 us -> 10.6 us  [send(): held = lax.all_to_all(packed, 'seq', 0, 0, tiled=True)]
    pallas_call x2 -> x0, local copies, waits for them, and re-layouts: 3.44 us -> none  [shards(): pl.pallas_call(functools.partial(kernel, chunk), grid_spec=pltpu.Prefetch...]
    slice x2 -> x0, local copies, waits for them, and re-layouts: 1.75 us -> none  [the longest x1 1.7 us: shards(): parts.append(queries[:, d * own * HD:(d + 1) * own * HD])]
  transfers between devices with their start and end apart: 1 -> 2, of which waited for: 1 -> 1; matrix products, arithmetic and copies ran while one was open for 4% -> 0% of each run, Pallas kernels for 0% -> 28%
where the time goes in v2:
time: 138 us; the launch traced here: 137 us
  Pallas kernels  78.8 us (57%)
  waiting for transfers between devices  43.7 us (32%)
  starting transfers between devices  10.6 us (8%)
  local copies, waits for them, and re-layouts  2.44 us (2%)
    pallas_call x2, Pallas kernels, run(): pl.pallas_call(functools.partial(kernel, chunk), grid_spec=pltpu.Prefetch...  67.9 us
    all_to_all x2, waiting for transfers between devices, send(): held = lax.all_to_all(packed, 'seq', 0, 0, tiled=True)  43.7 us
    pallas_call x2, Pallas kernels, pack(): pl.pallas_call(body, grid=(devices,), in_specs=[pl.BlockSpec((tok, count...  10.9 us
    all_to_all x2, starting transfers between devices, send(): held = lax.all_to_all(packed, 'seq', 0, 0, tiled=True)  10.6 us
  transfers between devices with their start and end apart: 2, of which 1 were waited for; matrix products, arithmetic and copies ran while one was open for 0% of the time, Pallas kernels for 28%

profile of v2, /device:TPU:0, one launch (start us, length us, event | category | flops | bytes accessed | tf_op | source)
XLA Modules:
  0.0 137.0 jit_solution(12728103849001096431)
XLA Ops:
  0.6 5.6 %shard_map.68 = bf16[8,256,512]{2,1,0:T(8,128)(2,1)} custom-call(bf16[256,4096]{1,0:T(8,128)(2,1)} %refs_0_.3, bf16[256,256]{1,0:T(8,128)(2,1)} %refs_1_.1, bf16[256,256]{1,0:T(8,128)(2,1)} %refs_2_.1), custom_call_target="tpu_custom_call" | custom-call | tf_op jit(solution)/shard_map/pallas_call | solution.py:188
  6.3 6.4 %all-to-all-start = ((bf16[8,256,512]{2,1,0:T(8,128)(2,1)}), bf16[8,256,512]{2,1,0:T(8,128)(2,1)S(1)}, u32[]{:S(2)}, u32[]{:S(2)}) async-start(bf16[8,256,512]{2,1,0:T(8,128)(2,1)} %shard_map.68), calls=%async_computation | async-start | bytes 4194304 | tf_op jit(solution)/shard_map/all_to_all | solution.py:202
  12.6 0.0 copy-start
  12.6 5.3 %shard_map.70 = bf16[8,256,256]{2,1,0:T(8,128)(2,1)} custom-call(bf16[256,4096]{1,0:T(8,128)(2,1)} %refs_0_.3), custom_call_target="tpu_custom_call" | custom-call | tf_op jit(solution)/shard_map/pallas_call | solution.py:188
  17.9 43.7 %all-to-all-done = bf16[8,256,512]{2,1,0:T(8,128)(2,1)S(1)} async-done(((bf16[8,256,512]{2,1,0:T(8,128)(2,1)}), bf16[8,256,512]{2,1,0:T(8,128)(2,1)S(1)}, u32[]{:S(2)}, u32[]{:S(2)}) %all-to-all-start) | async-done | bytes 2097184 | tf_op jit(solution)/shard_map/all_to_all | solution.py:202
  61.6 4.2 %all-to-all-start.1 = ((bf16[8,256,256]{2,1,0:T(8,128)(2,1)}), bf16[8,256,256]{2,1,0:T(8,128)(2,1)}, u32[]{:S(2)}, u32[]{:S(2)}) async-start(bf16[8,256,256]{2,1,0:T(8,128)(2,1)} %shard_map.70), calls=%async_computation.1 | async-start | bytes 2097152 | tf_op jit(solution)/shard_map/all_to_all | solution.py:202
  65.9 0.0 copy-done
  65.9 0.0 copy-start.1
  65.9 1.2 copy-done.1
  67.1 33.7 %shard_map.69 = (f32[2,64,128]{2,1,0:T(8,128)S(1)}, f32[2,64,128]{2,1,0:T(8,128)S(1)}) custom-call(s32[1]{0:T(128)} %bitcast.pos_ref, bf16[2048,512]{1,0:T(8,128)(2,1)S(1)} %bitcast.9, bf16[2048,512]{1,0:T(8,128)(2,1)S(1)} %bitcast.10, bf16[2048,512]{1,0:T(8,128)(2,1)S(1)} %bitcast.11, f32[32,64,128]{2,1,0:T(8,128)S(1)} %bitcast.14, f32[32,64,128]{2,1,0:T(8,128)S(1)} %bitcast.16), custom_call_target="tpu_custom_call" | custom-call | tf_op jit(solution)/shard_map/pallas_call | solution.py:210
  100.9 0.0 all-to-all-done.1
  100.9 0.0 copy-start.2
  100.9 1.2 copy-done.2
  102.1 34.2 %shard_map.71 = (f32[2,64,128]{2,1,0:T(8,128)S(1)}, f32[2,64,128]{2,1,0:T(8,128)S(1)}) custom-call(s32[1]{0:T(128)} %bitcast.pos_ref, bf16[2048,256]{1,0:T(8,128)(2,1)} %bitcast.4.q_ref, bf16[2048,512]{1,0:T(8,128)(2,1)S(1)} %bitcast.12, bf16[2048,512]{1,0:T(8,128)(2,1)S(1)} %bitcast.13, f32[32,64,128]{2,1,0:T(8,128)S(1)} %bitcast.15, ...), custom_call_target="tpu_custom_call" | custom-call | tf_op jit(solution)/shard_map/pallas_call | solution.py:210
  136.3 0.7 maximum_bitcast_fusion
Async XLA Ops:
  6.3 55.4 %all-to-all-start = ((bf16[8,256,512]{2,1,0:T(8,128)(2,1)}), bf16[8,256,512]{2,1,0:T(8,128)(2,1)S(1)}, u32[]{:S(2)}, u32[]{:S(2)}) async-start(bf16[8,256,512]{2,1,0:T(8,128)(2,1)} %shard_map.68), calls=%async_computation | async-start | bytes 4194304 | tf_op jit(solution)/shard_map/all_to_all | solution.py:202
  12.6 53.3 %copy-start = (f32[32,128,64]{1,2,0:T(8,128)S(1)}, f32[32,128,64]{1,2,0:T(8,128)}, u32[]{:S(2)}) copy-start(f32[32,128,64]{1,2,0:T(8,128)} %param.8) | copy-start | bytes 3145732
  61.6 39.2 %all-to-all-start.1 = ((bf16[8,256,256]{2,1,0:T(8,128)(2,1)}), bf16[8,256,256]{2,1,0:T(8,128)(2,1)}, u32[]{:S(2)}, u32[]{:S(2)}) async-start(bf16[8,256,256]{2,1,0:T(8,128)(2,1)} %shard_map.70), calls=%async_computation.1 | async-start | bytes 2097152 | tf_op jit(solution)/shard_map/all_to_all | solution.py:202
  65.9 1.2 copy-start.1
  100.9 1.2 copy-start.2
